TPU v7x, 32 devices: a whole 2x2x4 slice. The times are simulated.
32 devices in a mesh: dp: 2 (over x), row: 4 (over y, core), col: 4 (over z).
Axes of the slice: x: 2, y: 2, z: 4, core: 2. Of those that a mesh axis runs over, the one named last changes fastest.
Arguments:
- latents: float32 [24, 32, 128], P(('dp', 'row')), may hold values from -6 to 6
- labels: int32 [24], P(('dp', 'row')), may hold values from 0 to 999
- step_index: int32 [24], P(('dp', 'row')), may hold values from 1 to 8
- seeds: int32 [24], P(('dp', 'row')), may hold values from 0 to 2147483646
- class_table: bfloat16 [1000, 1152], replicated, may hold values from -6 to 6
- teacher_patch: bfloat16 [16, 1152], replicated, may hold values from -1.5 to 1.5
- teacher_mod: bfloat16 [1152, 3, 1152], P(('dp', 'row'), None, 'col'), may hold values from -0.1875 to 0.1875
- teacher_up: bfloat16 [1152, 4608], P(('dp', 'row'), 'col'), may hold values from -0.1875 to 0.1875
- teacher_down: bfloat16 [1152, 4608], P(('dp', 'row'), 'col'), may hold values from -0.09375 to 0.09375
- teacher_out: bfloat16 [16, 1152], replicated, may hold values from -0.1875 to 0.1875
- student_patch: bfloat16 [16, 1152], replicated, may hold values from -1.5 to 1.5
- student_mod: bfloat16 [1152, 3, 1152], P(('dp', 'row'), None, 'col'), may hold values from -0.1875 to 0.1875
- student_up: bfloat16 [1152, 4608], P(('dp', 'row'), 'col'), may hold values from -0.1875 to 0.1875
- student_down: bfloat16 [1152, 4608], P(('dp', 'row'), 'col'), may hold values from -0.09375 to 0.09375
- student_out: bfloat16 [16, 1152], replicated, may hold values from -0.1875 to 0.1875
Outputs:
- up_gradient: float32 [1152, 4608], P(('dp', 'row'), 'col')
- down_gradient: float32 [1152, 4608], P(('dp', 'row'), 'col')
All inputs are finite; a program needn't handle non-finite values.
Results may differ from a plain program's by a relative error of at most 0.002.
Values may be sent and summed in bfloat16 or wider, within the bound.
No kernel may reach another device: no remote copies, remote signals or barrier semaphores. Data moves between devices by JAX's collectives and lax.ppermute only.
A program may use at most 128 MiB of HBM per device.

v0:
```python
import math
import jax
import jax.numpy as jnp
from jax import lax
from jax.sharding import PartitionSpec as P

D = 1152
CLASSES = 1000
SEQ = 256
PATCH = 16
STEPS = 8
HALF_PI = 0.5 * math.pi
ROOT_TWO_PI = math.sqrt(2.0 / math.pi)


def plan(times):
    return (jnp.cos(HALF_PI * times), jnp.sin(HALF_PI * times))


def mixing(value):
    amount = jnp.int32(16)
    value = value ^ lax.shift_right_logical(value, amount)
    value = value * 73244475
    value = value ^ lax.shift_right_logical(value, amount)
    value = value * 73244475
    value = value ^ lax.shift_right_logical(value, amount)
    return value


def noise_of(seeds):
    total = SEQ * PATCH
    places = jnp.arange(total, dtype=jnp.int32).reshape(1, total // 128, 128)
    mixed = mixing(seeds[:, None, None] * 1103515245 + places * 40503 + 12345)
    uniform = (lax.shift_right_logical(mixed, jnp.int32(8)).astype(jnp.float32) + 0.5) * (
        1.0 / 16777216.0
    )
    return math.sqrt(2.0) * lax.erf_inv(2.0 * uniform - 1.0)


def time_features(times):
    half = D // 2
    freqs = jnp.exp(-math.log(10000.0) * jnp.arange(half, dtype=jnp.float32) / half)
    angle = (1000.0 * times)[:, None] * freqs[None, :]
    return jnp.concatenate([jnp.cos(angle), jnp.sin(angle)], axis=1)


def condition(times, labels, class_table):
    onehot = (labels[:, None] == jnp.arange(CLASSES, dtype=jnp.int32)[None, :]).astype(jnp.bfloat16)
    embedded = jnp.dot(onehot, class_table, preferred_element_type=jnp.float32)
    return jax.nn.silu(embedded + time_features(times)).astype(jnp.bfloat16)


def positions():
    quarter = D // 4
    omega = 1.0 / 10000.0 ** (jnp.arange(quarter, dtype=jnp.float32) / quarter)
    side = math.isqrt(SEQ)
    cells = jnp.arange(SEQ, dtype=jnp.int32)
    grid_row = (cells // side).astype(jnp.float32)
    grid_col = (cells % side).astype(jnp.float32)
    row_angle = grid_row[:, None] * omega[None, :]
    col_angle = grid_col[:, None] * omega[None, :]
    return jnp.concatenate(
        [jnp.sin(row_angle), jnp.cos(row_angle), jnp.sin(col_angle), jnp.cos(col_angle)], axis=1
    )


def layer_norm(values):
    center = values - jnp.mean(values, axis=-1, keepdims=True)
    spread = jnp.mean(center * center, axis=-1, keepdims=True)
    reciprocal = lax.rsqrt(spread + 1e-06)
    return (center * reciprocal, reciprocal)


def gelu_slope(pre):
    inner = ROOT_TWO_PI * (pre + 0.044715 * pre * pre * pre)
    tangent = jnp.tanh(inner)
    return 0.5 * (1.0 + tangent) + 0.5 * pre * (1.0 - tangent * tangent) * ROOT_TWO_PI * (
        1.0 + 3.0 * 0.044715 * pre * pre
    )


def contract_last(left, right):
    return lax.dot_general(
        left, right, (((1,), (1,)), ((), ())), preferred_element_type=jnp.float32
    )


def contract_first(left, right):
    return lax.dot_general(
        left, right, (((0,), (0,)), ((), ())), preferred_element_type=jnp.float32
    )


def network(state, mods, patch_weight, out_weight, pos, up_product, down_product):
    samples = state.shape[0]
    tokens = state.reshape(samples * SEQ, PATCH).astype(jnp.bfloat16)
    base = (
        jnp.dot(tokens, patch_weight, preferred_element_type=jnp.float32).reshape(samples, SEQ, D)
        + pos[None]
    )
    shift = mods[:, 0][:, None, :]
    scale = mods[:, 1][:, None, :]
    gate = mods[:, 2][:, None, :]
    normed, _ = layer_norm(base)
    act = (normed * (1.0 + scale) + shift).astype(jnp.bfloat16).reshape(samples * SEQ, D)
    pre = up_product(act)
    hidden = jax.nn.gelu(pre, approximate=True).astype(jnp.bfloat16)
    partial_out = down_product(hidden).astype(jnp.bfloat16)
    mixed = lax.psum(partial_out, "col").astype(jnp.float32)
    later = base + gate * mixed.reshape(samples, SEQ, D)
    final, reciprocal = layer_norm(later)
    velocity = contract_last(final.astype(jnp.bfloat16).reshape(samples * SEQ, D), out_weight)
    return (
        velocity.reshape(samples, SEQ * PATCH // 128, 128),
        (act, pre, hidden, final, reciprocal, gate, out_weight),
    )


def reduce_gradient(left, right):
    return lax.psum_scatter(
        contract_first(left, right), ("dp", "row"), scatter_dimension=0, tiled=True
    )


def body(
    latents,
    labels,
    step_index,
    seeds,
    class_table,
    teacher_patch,
    teacher_mod,
    teacher_up,
    teacher_down,
    teacher_out,
    student_patch,
    student_mod,
    student_up,
    student_down,
    student_out,
):
    samples = latents.shape[0]
    batch_total = samples * lax.axis_size(("dp", "row"))
    pos = positions()
    all_labels, all_steps = (
        lax.all_gather(labels, ("dp", "row"), axis=0, tiled=True),
        lax.all_gather(step_index, ("dp", "row"), axis=0, tiled=True),
    )
    all_now = all_steps.astype(jnp.float32) / STEPS
    cond_now = condition(all_now, all_labels, class_table)
    cond_mid = condition(all_now - 0.5 / STEPS, all_labels, class_table)
    own_rows = teacher_mod.shape[0]
    offset = lax.axis_index(("dp", "row")) * own_rows
    rows_now = lax.dynamic_slice_in_dim(cond_now, offset, own_rows, 1)
    rows_mid = lax.dynamic_slice_in_dim(cond_mid, offset, own_rows, 1)
    teacher_part = jnp.einsum(
        "nkd,dcf->nkcf",
        jnp.stack([rows_now, rows_mid], axis=1),
        teacher_mod,
        preferred_element_type=jnp.float32,
    )
    student_part = jnp.einsum(
        "nd,dcf->ncf", rows_now, student_mod, preferred_element_type=jnp.float32
    )[:, None]
    teacher_sums, student_sums = (
        lax.psum_scatter(teacher_part, ("dp", "row"), scatter_dimension=0, tiled=True),
        lax.psum_scatter(student_part, ("dp", "row"), scatter_dimension=0, tiled=True),
    )
    teacher_mods, student_mods = (
        lax.all_gather(teacher_sums, "col", axis=3, tiled=True),
        lax.all_gather(student_sums, "col", axis=3, tiled=True),
    )
    now = step_index.astype(jnp.float32) / STEPS
    alpha, sigma = plan(now[:, None, None])
    alpha_mid, sigma_mid = plan((now - 0.5 / STEPS)[:, None, None])
    alpha_end, sigma_end = plan((now - 1.0 / STEPS)[:, None, None])
    noisy = alpha * latents + sigma * noise_of(seeds)
    up_panel, down_panel = (
        lax.all_gather(teacher_up, ("dp", "row"), axis=0, tiled=True),
        lax.all_gather(teacher_down, ("dp", "row"), axis=0, tiled=True),
    )

    def teacher_up_product(act):
        return jnp.dot(act, up_panel, preferred_element_type=jnp.float32)

    def teacher_down_product(hidden):
        return contract_last(hidden, down_panel)

    first_v, _ = network(
        noisy,
        teacher_mods[:, 0],
        teacher_patch,
        teacher_out,
        pos,
        teacher_up_product,
        teacher_down_product,
    )
    first_x = alpha * noisy - sigma * first_v
    halfway = alpha_mid * first_x + sigma_mid * (noisy - alpha * first_x) / sigma
    second_v, _ = network(
        halfway,
        teacher_mods[:, 1],
        teacher_patch,
        teacher_out,
        pos,
        teacher_up_product,
        teacher_down_product,
    )
    second_x = alpha_mid * halfway - sigma_mid * second_v
    landing = alpha_end * second_x + sigma_end * (halfway - alpha_mid * second_x) / sigma_mid
    ratio = sigma_end / sigma
    target = (landing - ratio * noisy) / (alpha_end - ratio * alpha)

    def student_up_product(act):
        return jnp.dot(
            act,
            lax.all_gather(student_up, ("dp", "row"), axis=0, tiled=True),
            preferred_element_type=jnp.float32,
        )

    student_panel = lax.all_gather(student_down, ("dp", "row"), axis=0, tiled=True)

    def student_down_product(hidden):
        return contract_last(hidden, student_panel)

    student_v, saved = network(
        noisy,
        student_mods[:, 0],
        student_patch,
        student_out,
        pos,
        student_up_product,
        student_down_product,
    )
    student_x = alpha * noisy - sigma * student_v
    weight = jnp.maximum(alpha * alpha / (sigma * sigma), 1.0)
    back_velocity = (-2.0 * sigma * weight * (student_x - target) / batch_total).reshape(
        samples * SEQ, PATCH
    )
    act, pre, hidden, final, reciprocal, gate_share, out_share = saved
    back_final = jnp.dot(
        back_velocity, out_share.astype(jnp.float32), precision=lax.Precision.HIGHEST
    ).reshape(samples, SEQ, -1)
    centre = jnp.mean(back_final, axis=2, keepdims=True)
    along = jnp.mean(back_final * final, axis=2, keepdims=True)
    back_mixed = (
        (gate_share * (reciprocal * (back_final - centre - final * along)))
        .astype(jnp.bfloat16)
        .reshape(samples * SEQ, D)
    )
    down_gradient = reduce_gradient(back_mixed, hidden)
    back_hidden = jnp.dot(back_mixed, student_panel, preferred_element_type=jnp.float32)
    back_pre = (back_hidden * gelu_slope(pre)).astype(jnp.bfloat16)
    up_gradient = reduce_gradient(act, back_pre)
    return (up_gradient, down_gradient)


def solution(mesh):
    placed = (
        P(("dp", "row"), None, None),
        P(("dp", "row")),
        P(("dp", "row")),
        P(("dp", "row")),
        P(),
        P(),
        P(("dp", "row"), None, "col"),
        P(("dp", "row"), "col"),
        P(("dp", "row"), "col"),
        P(),
        P(),
        P(("dp", "row"), None, "col"),
        P(("dp", "row"), "col"),
        P(("dp", "row"), "col"),
        P(),
    )
    return jax.shard_map(
        body,
        mesh=mesh,
        in_specs=placed,
        out_specs=(P(("dp", "row"), "col"), P(("dp", "row"), "col")),
        check_vma=False,
    )
```

profile of v0, /device:TPU:0, one launch (start us, length us, event | category | flops | bytes accessed | tf_op | source)
XLA Modules:
  0.0 598.2 jit_solution(1822111172915230698)
XLA Ops:
  7.3 1.5 fusion.98
  11.2 9.5 %all-reduce.4 = (s32[24]{0:T(128)S(1)}, s32[24]{0:T(128)S(1)}) all-reduce(s32[24]{0:T(128)S(1)} %dynamic-update-slice, s32[24]{0:T(128)S(1)} %dynamic-update-slice.1), channel_id=1, replica_groups=mesh['dp'=2,'row'=4,'col'=4] {'dp','row'}, use_global_device_ids=true, to_apply=%add | all-reduce | flops 48 | bytes 384
  21.9 1.2 fusion.43
  30.0 2.8 multiply_cosine_fusion
  32.8 1.4 concatenate.9
  34.2 2.2 fusion.100
  37.5 2.4 fusion.99
  40.5 2.5 multiply_reduce_fusion.6
  44.3 33.5 %all-reduce.13.cloned.1.call-done = (f32[24,1,3,288]{3,1,2,0:T(1,128)}, f32[24,2,3,288]{3,1,2,0:T(2,128)}) async-done(((f32[24,1,3,288]{3,1,2,0:T(1,128)}, f32[24,2,3,288]{3,1,2,0:T(2,128)}), (f32[24,1,3,288]{3,1,2,0:T(1,128)}, f32[24,2,3,288]{3,1,2,0:T(2,128)})) %all-reduce.13.cloned.1.call-update) | async-done | bytes 248848
  77.9 1.4 constant_dynamic-slice_fusion
  79.2 2.0 copy.57
  81.2 62.1 %all_gather.29 = f32[3,2,3,1152]{2,1,0,3:T(2,128)S(1)} all-gather(f32[3,2,3,288]{2,1,0,3:T(2,128)} %copy.57), channel_id=1, replica_groups=mesh['dp'=2,'row'=4,'col'=4] {'col'}, dimensions={3}, use_global_device_ids=true | all-gather | bytes 103680 | tf_op jit(solution)/shard_map/all_gather | solution.py:170
  143.3 3.9 fusion.94
  147.1 4.6 copy.81
  151.7 4.6 copy.82
  157.0 1.1 copy.52
  158.0 38.8 %all_gather.26 = f32[3,1,3,1152]{2,1,0,3:T(1,128)} all-gather(f32[3,1,3,288]{2,1,0,3:T(1,128)} %copy.52), channel_id=1, replica_groups=mesh['dp'=2,'row'=4,'col'=4] {'col'}, dimensions={3}, use_global_device_ids=true | all-gather | bytes 51840 | tf_op jit(solution)/shard_map/all_gather | solution.py:171
  196.9 4.6 copy.53
  201.4 1.6 fusion.97
  203.0 1.0 fusion.95
  204.0 3.1 add_convert_fusion.1
  207.2 4.5 add_convert_fusion.2
  211.7 9.5 %convolution_convert_fusion.1 = bf16[768,1152]{1,0:T(8,128)(2,1)} fusion(bf16[1152,1152]{1,0:T(8,128)(2,1)} %all-gather.11.cloned.1.call-done, bf16[768,1152]{1,0:T(8,128)(2,1)} %bitcast.116, bf16[1152,1152]{1,0:T(8,128)(2,1)} %all-gather.9.cloned.1.call-done), kind=kOutput, calls=%fused_computation.56 | convolution fusion | flops 4085710848 | bytes 8847360 | tf_op jit(solution)/shard_map/dot_general | solution.py:83
  221.4 1.6 fusion.96
  223.0 1.3 copy.93
  225.0 6.7 %fusion.106 = f32[768,1152]{1,0:T(8,128)} fusion(bf16[768,1152]{1,0:T(8,128)(2,1)} %bitcast.109, bf16[1152,1152]{1,0:T(8,128)(2,1)} %all-gather.5.cloned.1.call-done), kind=kOutput, calls=%fused_computation.198 | convolution fusion | flops 2038431744 | bytes 7962624 | tf_op jit(solution)/shard_map/dot_general | solution.py:215
  231.7 7.3 %convolution_convert_fusion.2 = bf16[768,1152]{1,0:T(8,128)(2,1)} fusion(bf16[1152,1152]{1,0:T(8,128)(2,1)} %all-gather.7.cloned.1.call-done, f32[768,1152]{1,0:T(8,128)} %fusion.106), kind=kOutput, calls=%fused_computation.57 | convolution fusion | flops 2047279104 | bytes 7962624 | tf_op jit(solution)/shard_map/dot_general | solution.py:83
  238.9 54.8 %all-reduce.11.cloned.1.call-done = bf16[3,256,1152]{2,1,0:T(8,128)(2,1)} async-done(((bf16[3,256,1152]{2,1,0:T(8,128)(2,1)}), bf16[3,256,1152]{2,1,0:T(8,128)(2,1)}) %all-reduce.11.cloned.1.call-update) | async-done | bytes 1769488 | tf_op jit(solution)/shard_map/psum | solution.py:109
  293.8 2.1 fusion.41
  298.3 0.9 fusion.86
  300.1 2.1 fusion.101
  302.7 2.4 add_convert_fusion
  305.2 9.7 %convolution_convert_fusion = bf16[768,1152]{1,0:T(8,128)(2,1)} fusion(bf16[1152,1152]{1,0:T(8,128)(2,1)} %all-gather.11.cloned.1.call-done, bf16[768,1152]{1,0:T(8,128)(2,1)} %bitcast.117, bf16[1152,1152]{1,0:T(8,128)(2,1)} %all-gather.9.cloned.1.call-done), kind=kOutput, calls=%fused_computation.55 | convolution fusion | flops 4085710848 | bytes 8847360 | tf_op jit(solution)/shard_map/dot_general | solution.py:83
  315.6 1.3 copy.92
  316.9 131.0 %all-reduce.15.cloned.1.call-done = (bf16[3,256,1152]{2,1,0:T(8,128)(2,1)}, bf16[3,256,1152]{2,1,0:T(8,128)(2,1)}) async-done(((bf16[3,256,1152]{2,1,0:T(8,128)(2,1)}, bf16[3,256,1152]{2,1,0:T(8,128)(2,1)}), (bf16[3,256,1152]{2,1,0:T(8,128)(2,1)}, bf16[3,256,1152]{2,1,0:T(8,128)(2,1)})) %all-reduce.15.cloned.1.call-update) | async-done | bytes 3538960 | tf_op jit(solution)/shard_map/psum | solution.py:109
  447.9 3.1 fusion.92
  451.5 1.3 copy-done.2
  453.2 1.3 fusion.107
  454.5 1.8 reshape.244
  456.3 2.1 fusion.42
  460.8 1.0 multiply_multiply_fusion.4
  462.0 4.6 fusion.90
  466.7 1.4 multiply_convert_fusion
  468.0 1.2 copy-done.8
  469.2 5.0 fusion.87
  474.6 12.3 %fusion.110 = f32[1152,1152]{1,0:T(8,128)} fusion(bf16[768,1152]{1,0:T(8,128)(2,1)} %bitcast.110, f32[768,1152]{1,0:T(8,128)} %fusion.106, bf16[768,1152]{1,0:T(8,128)(2,1)} %bitcast.115, bf16[1152,1152]{1,0:T(8,128)(2,1)} %all-gather.7.cloned.1.call-done), kind=kOutput, calls=%fused_computation.202 | convolution fusion | flops 4093673472 | bytes 15040512 | tf_op jit(solution)/shard_map/dot_general | solution.py:89
  486.9 43.4 %reduce-scatter.5.cloned.1.call-done = f32[144,1152]{1,0:T(8,128)} async-done(((f32[1152,1152]{1,0:T(8,128)}), f32[144,1152]{1,0:T(8,128)}) %reduce-scatter.5.cloned.1.call-update) | async-done | bytes 663568 | tf_op jit(solution)/shard_map/reduce_scatter | solution.py:120
  530.3 60.9 %reduce-scatter.3.cloned.1.call-done = f32[144,1152]{1,0:T(8,128)} async-done(((f32[1152,1152]{1,0:T(8,128)}), f32[144,1152]{1,0:T(8,128)}) %reduce-scatter.3.cloned.1.call-update) | async-done | bytes 663568 | tf_op jit(solution)/shard_map/reduce_scatter | solution.py:120
  (135 shorter events, 21.8 us)
Async XLA Ops:
  7.2 14.0 %copy-start = (bf16[1000,1152]{1,0:T(8,128)(2,1)S(1)}, bf16[1000,1152]{1,0:T(8,128)(2,1)}, u32[]{:S(2)}) copy-start(bf16[1000,1152]{1,0:T(8,128)(2,1)} %param.19) | copy-start | bytes 6912004
  7.2 20.4 %copy-start.28 = (s32[3]{0:T(128)S(1)}, s32[3]{0:T(128)}, u32[]{:S(2)}) copy-start(s32[3]{0:T(128)} %param.17) | copy-start | bytes 40
  7.2 16.6 %copy-start.10 = (bf16[144,3,288]{2,0,1:T(8,128)(2,1)S(1)}, bf16[144,3,288]{2,0,1:T(8,128)(2,1)}, u32[]{:S(2)}) copy-start(bf16[144,3,288]{2,0,1:T(8,128)(2,1)} %param.26) | copy-start | bytes 746500
  7.2 21.1 %copy-start.29 = (s32[3]{0:T(128)S(1)}, s32[3]{0:T(128)}, u32[]{:S(2)}) copy-start(s32[3]{0:T(128)} %param.18) | copy-start | bytes 40
  7.2 21.1 %copy-start.19 = (f32[3,32,128]{2,1,0:T(8,128)S(1)}, f32[3,32,128]{2,1,0:T(8,128)}, u32[]{:S(2)}) copy-start(f32[3,32,128]{2,1,0:T(8,128)} %param.15) | copy-start | bytes 147460
  7.2 70.6 %all-reduce.13.cloned.1.call-start = ((), (), s32[]{:S(2)}) async-start(), calls=%async_computation.9 | async-start | bytes 663552
  24.9 186.8 %all-gather.11.cloned.1.call-start = ((), (), s32[]{:S(2)}) async-start(), calls=%async_computation.5 | async-start | bytes 2985984 | tf_op jit(solution)/shard_map/all_gather | solution.py:180
  25.6 186.1 %all-gather.9.cloned.1.call-start = ((), (), s32[]{:S(2)}) async-start(), calls=%async_computation.4 | async-start | bytes 2985984 | tf_op jit(solution)/shard_map/all_gather | solution.py:179
  26.4 198.6 %all-gather.5.cloned.1.call-start = ((), (), s32[]{:S(2)}) async-start(), calls=%async_computation.2 | async-start | bytes 2985984 | tf_op jit(solution)/shard_map/all_gather | solution.py:217
  27.0 204.7 %all-gather.7.cloned.1.call-start = ((), (), s32[]{:S(2)}) async-start(), calls=%async_computation.3 | async-start | bytes 2985984 | tf_op jit(solution)/shard_map/all_gather | solution.py:221
  27.5 266.3 %all-reduce.11.cloned.1.call-start = ((), (), s32[]{:S(2)}) async-start(), calls=%async_computation.6 | async-start | bytes 3538944 | tf_op jit(solution)/shard_map/psum | solution.py:109
  28.3 1.7 copy-start.25
  34.2 3.3 copy-start.4
  34.2 3.3 copy-start.7
  34.2 3.3 copy-start.20
  36.4 3.5 copy-start.21
  39.9 0.6 copy-start.22
  201.4 5.7 copy-start.23
  201.4 5.7 copy-start.24
  221.2 226.7 %all-reduce.15.cloned.1.call-start = ((), (), s32[]{:S(2)}) async-start(), calls=%async_computation.10 | async-start | bytes 7077888 | tf_op jit(solution)/shard_map/psum | solution.py:109
  293.8 2.2 copy-start.6
  293.8 2.2 copy-start.12
  296.8 0.8 copy-start.15
  298.3 0.9 copy-start.9
  300.1 2.6 copy-start.17
  300.1 2.6 copy-start.18
  314.9 215.4 %reduce-scatter.5.cloned.1.call-start = ((), (), s32[]{:S(2)}) async-start(), calls=%async_computation.8 | async-start | bytes 5971968 | tf_op jit(solution)/shard_map/reduce_scatter | solution.py:120
  451.0 1.8 copy-start.2
  451.5 1.7 copy-start.14
  456.3 2.2 copy-start.5
  456.3 2.2 copy-start.11
  459.2 0.8 copy-start.16
  459.3 1.5 copy-start.26
  459.3 1.5 copy-start.27
  462.0 4.7 copy-start.3
  462.0 4.7 copy-start.13
  466.6 2.6 copy-start.30
  468.0 1.2 copy-start.8
  474.3 116.9 %reduce-scatter.3.cloned.1.call-start = ((), (), s32[]{:S(2)}) async-start(), calls=%async_computation.7 | async-start | bytes 5971968 | tf_op jit(solution)/shard_map/reduce_scatter | solution.py:120
  474.6 116.6 %copy-start.1 = (bf16[1000,1152]{1,0:T(8,128)(2,1)S(1)}, bf16[1000,1152]{1,0:T(8,128)(2,1)}, u32[]{:S(2)}) copy-start(bf16[1000,1152]{1,0:T(8,128)(2,1)} %param.19) | copy-start | bytes 6912004
Sparse Core Ops, SparseCore 0:
  25.0 52.8 all-reduce.12
  79.7 30.7 all-gather.10
  112.4 30.1 all-gather.8
  144.3 30.1 all-gather.4
  176.2 30.1 all-gather.6
  221.3 72.3 all-reduce.10
  315.0 132.8 all-reduce.14
  474.4 55.8 reduce-scatter.4
  534.3 56.8 reduce-scatter.2
where the time goes:
time: 607 us; the launch traced here: 598 us
  waiting for transfers between devices  326 us (54%)
  blocking collectives  110 us (18%)
  matrix products  66.2 us (11%)
  local copies, waits for them, and re-layouts  39.9 us (7%)
  other arithmetic  38.5 us (6%)
  between operations  16.2 us (3%)
    psum x2, waiting for transfers between devices, network(): mixed = lax.psum(partial_out, 'col').astype(jnp.float32)  186 us
    reduce_scatter x2, waiting for transfers between devices, reduce_gradient(): lax.psum_scatter(contract_first(left, right), ('dp', 'row'), scatter_dime...  104 us
    all_gather x1, blocking collectives, body(): lax.all_gather(teacher_sums, 'col', axis=3, tiled=True)  62.1 us
    all_gather x1, blocking collectives, body(): lax.all_gather(student_sums, 'col', axis=3, tiled=True)  38.8 us
    unnamed x10, waiting for transfers between devices  36.1 us
    dot_general x6, matrix products, contract_last(): lax.dot_general(left, right, (((1,), (1,)), ((), ())), preferred_element_...  29 us
    unnamed x77, local copies, waits for them, and re-layouts  21.6 us
    dot_general x2, matrix products, contract_first(): lax.dot_general(left, right, (((0,), (0,)), ((), ())), preferred_element_...  17.3 us
  transfers between devices with their start and end apart: 9, of which 5 were waited for; matrix products, arithmetic and copies ran while one was open for 15% of the time, Pallas kernels for 0%

commit v1 on v0

--- a/solution.py
+++ b/solution.py
@@ -168,7 +168,7 @@
     )
     teacher_mods, student_mods = (
         lax.all_gather(teacher_sums, "col", axis=3, tiled=True),
-        lax.all_gather(student_sums, "col", axis=3, tiled=True),
+        jnp.concatenate(lax.all_gather(student_sums, "col"), axis=3),
     )
     now = step_index.astype(jnp.float32) / STEPS
     alpha, sigma = plan(now[:, None, None])

time: 607 us -> 597 us (0.984)
  blocking collectives: 110 us -> 85.7 us
  waiting for transfers between devices: 326 us -> 345 us
    all_gather x1, blocking collectives: 38.8 us -> 14.1 us  [body(): lax.all_gather(student_sums, 'col')]
    psum x2, waiting for transfers between devices: 186 us -> 202 us  [network(): mixed = lax.psum(partial_out, 'col').astype(jnp.float32)]
    unnamed x77 -> x72, local copies, waits for them, and re-layouts: 21.6 us -> 17.1 us
  transfers between devices with their start and end apart: 9 -> 9, of which waited for: 5 -> 6; matrix products, arithmetic and copies ran while one was open for 15% -> 15% of each run, Pallas kernels for 0% -> 0%
where the time goes in v1:
time: 597 us; the launch traced here: 589 us
  waiting for transfers between devices  345 us (58%)
  blocking collectives  85.7 us (14%)
  matrix products  66.4 us (11%)
  other arithmetic  38.5 us (6%)
  local copies, waits for them, and re-layouts  36.5 us (6%)
  between operations  16.1 us (3%)
    psum x2, waiting for transfers between devices, network(): mixed = lax.psum(partial_out, 'col').astype(jnp.float32)  202 us
    reduce_scatter x2, waiting for transfers between devices, reduce_gradient(): lax.psum_scatter(contract_first(left, right), ('dp', 'row'), scatter_dime...  104 us
    all_gather x1, blocking collectives, body(): lax.all_gather(teacher_sums, 'col', axis=3, tiled=True)  62.1 us
    unnamed x10, waiting for transfers between devices  36 us
    dot_general x6, matrix products, contract_last(): lax.dot_general(left, right, (((1,), (1,)), ((), ())), preferred_element_...  29.1 us
    dot_general x2, matrix products, contract_first(): lax.dot_general(left, right, (((0,), (0,)), ((), ())), preferred_element_...  17.4 us
    unnamed x72, local copies, waits for them, and re-layouts  17.1 us
    all_gather x1, blocking collectives, body(): lax.all_gather(student_sums, 'col')  14.1 us
  transfers between devices with their start and end apart: 9, of which 6 were waited for; matrix products, arithmetic and copies ran while one was open for 15% of the time, Pallas kernels for 0%

profile of v1, /device:TPU:0, one launch (start us, length us, event | category | flops | bytes accessed | tf_op | source)
XLA Modules:
  0.0 588.6 jit_solution(5190326969681787099)
XLA Ops:
  7.3 1.4 fusion.98
  11.1 9.5 %all-reduce.4 = (s32[24]{0:T(128)S(1)}, s32[24]{0:T(128)S(1)}) all-reduce(s32[24]{0:T(128)S(1)} %dynamic-update-slice, s32[24]{0:T(128)S(1)} %dynamic-update-slice.1), channel_id=1, replica_groups=mesh['dp'=2,'row'=4,'col'=4] {'dp','row'}, use_global_device_ids=true, to_apply=%add | all-reduce | flops 48 | bytes 384
  21.8 1.2 fusion.43
  29.9 2.8 multiply_cosine_fusion
  32.7 1.4 concatenate.9
  34.1 2.2 fusion.100
  37.4 2.5 fusion.99
  40.5 2.5 multiply_reduce_fusion.6
  44.3 33.5 %all-reduce.13.cloned.1.call-done = (f32[24,1,3,288]{3,1,2,0:T(1,128)}, f32[24,2,3,288]{3,1,2,0:T(2,128)}) async-done(((f32[24,1,3,288]{3,1,2,0:T(1,128)}, f32[24,2,3,288]{3,1,2,0:T(2,128)}), (f32[24,1,3,288]{3,1,2,0:T(1,128)}, f32[24,2,3,288]{3,1,2,0:T(2,128)})) %all-reduce.13.cloned.1.call-update) | async-done | bytes 248848
  77.8 1.4 constant_dynamic-slice_fusion
  79.1 2.0 copy.57
  81.1 62.1 %all_gather.33 = f32[3,2,3,1152]{2,1,0,3:T(2,128)S(1)} all-gather(f32[3,2,3,288]{2,1,0,3:T(2,128)} %copy.57), channel_id=1, replica_groups=mesh['dp'=2,'row'=4,'col'=4] {'col'}, dimensions={3}, use_global_device_ids=true | all-gather | bytes 103680 | tf_op jit(solution)/shard_map/all_gather | solution.py:170
  143.2 3.9 fusion.94
  147.1 4.6 copy.81
  151.6 4.6 copy.61
  156.9 14.1 %all-gather = f32[12,1,3,288]{3,1,2,0:T(1,128)S(1)} all-gather(f32[3,1,3,288]{3,1,2,0:T(1,128)S(1)} %constant_dynamic-slice_fusion.1), channel_id=2, replica_groups=mesh['dp'=2,'row'=4,'col'=4] {'col'}, dimensions={0}, use_global_device_ids=true | all-gather | bytes 51840 | tf_op jit(solution)/shard_map/all_gather | solution.py:171
  171.6 1.6 squeeze_reshape.3
  173.2 1.6 fusion.97
  174.7 1.0 fusion.95
  175.7 3.2 add_convert_fusion.1
  178.9 4.5 add_convert_fusion.2
  183.4 9.6 %convolution_convert_fusion.1 = bf16[768,1152]{1,0:T(8,128)(2,1)} fusion(bf16[1152,1152]{1,0:T(8,128)(2,1)} %all-gather.12.cloned.1.call-done, bf16[768,1152]{1,0:T(8,128)(2,1)} %bitcast.120, bf16[1152,1152]{1,0:T(8,128)(2,1)} %all-gather.10.cloned.1.call-done), kind=kOutput, calls=%fused_computation.56 | convolution fusion | flops 4085710848 | bytes 8847360 | tf_op jit(solution)/shard_map/dot_general | solution.py:83
  193.3 1.6 fusion.96
  194.8 1.3 copy.92
  196.8 6.7 %fusion.106 = f32[768,1152]{1,0:T(8,128)} fusion(bf16[768,1152]{1,0:T(8,128)(2,1)} %bitcast.113, bf16[1152,1152]{1,0:T(8,128)(2,1)} %all-gather.6.cloned.1.call-done), kind=kOutput, calls=%fused_computation.198 | convolution fusion | flops 2038431744 | bytes 7962624 | tf_op jit(solution)/shard_map/dot_general | solution.py:215
  203.5 2.7 all-gather.8.cloned.1.call-done
  206.2 7.2 %convolution_convert_fusion.2 = bf16[768,1152]{1,0:T(8,128)(2,1)} fusion(bf16[1152,1152]{1,0:T(8,128)(2,1)} %all-gather.8.cloned.1.call-done, f32[768,1152]{1,0:T(8,128)} %fusion.106), kind=kOutput, calls=%fused_computation.57 | convolution fusion | flops 2047279104 | bytes 7962624 | tf_op jit(solution)/shard_map/dot_general | solution.py:83
  213.5 70.5 %all-reduce.11.cloned.1.call-done = bf16[3,256,1152]{2,1,0:T(8,128)(2,1)} async-done(((bf16[3,256,1152]{2,1,0:T(8,128)(2,1)}), bf16[3,256,1152]{2,1,0:T(8,128)(2,1)}) %all-reduce.11.cloned.1.call-update) | async-done | bytes 1769488 | tf_op jit(solution)/shard_map/psum | solution.py:109
  284.0 2.1 fusion.41
  288.5 0.9 fusion.86
  290.3 2.1 fusion.101
  292.9 2.4 add_convert_fusion
  295.4 9.7 %convolution_convert_fusion = bf16[768,1152]{1,0:T(8,128)(2,1)} fusion(bf16[1152,1152]{1,0:T(8,128)(2,1)} %all-gather.12.cloned.1.call-done, bf16[768,1152]{1,0:T(8,128)(2,1)} %bitcast.121, bf16[1152,1152]{1,0:T(8,128)(2,1)} %all-gather.10.cloned.1.call-done), kind=kOutput, calls=%fused_computation.55 | convolution fusion | flops 4085710848 | bytes 8847360 | tf_op jit(solution)/shard_map/dot_general | solution.py:83
  305.8 1.3 copy.91
  307.1 131.0 %all-reduce.15.cloned.1.call-done = (bf16[3,256,1152]{2,1,0:T(8,128)(2,1)}, bf16[3,256,1152]{2,1,0:T(8,128)(2,1)}) async-done(((bf16[3,256,1152]{2,1,0:T(8,128)(2,1)}, bf16[3,256,1152]{2,1,0:T(8,128)(2,1)}), (bf16[3,256,1152]{2,1,0:T(8,128)(2,1)}, bf16[3,256,1152]{2,1,0:T(8,128)(2,1)})) %all-reduce.15.cloned.1.call-update) | async-done | bytes 3538960 | tf_op jit(solution)/shard_map/psum | solution.py:109
  438.1 3.1 fusion.92
  441.7 1.4 copy-done.2
  443.5 1.3 fusion.107
  444.8 1.8 reshape.248
  446.6 2.1 fusion.42
  451.1 1.0 multiply_multiply_fusion.4
  452.3 4.6 fusion.90
  457.0 1.4 multiply_convert_fusion
  458.4 1.2 copy-done.8
  459.6 5.1 fusion.87
  465.0 12.3 %fusion.110 = f32[1152,1152]{1,0:T(8,128)} fusion(bf16[768,1152]{1,0:T(8,128)(2,1)} %bitcast.114, f32[768,1152]{1,0:T(8,128)} %fusion.106, bf16[768,1152]{1,0:T(8,128)(2,1)} %bitcast.119, bf16[1152,1152]{1,0:T(8,128)(2,1)} %all-gather.8.cloned.1.call-done), kind=kOutput, calls=%fused_computation.202 | convolution fusion | flops 4093673472 | bytes 15040512 | tf_op jit(solution)/shard_map/dot_general | solution.py:89
  477.3 43.4 %reduce-scatter.5.cloned.1.call-done = f32[144,1152]{1,0:T(8,128)} async-done(((f32[1152,1152]{1,0:T(8,128)}), f32[144,1152]{1,0:T(8,128)}) %reduce-scatter.5.cloned.1.call-update) | async-done | bytes 663568 | tf_op jit(solution)/shard_map/reduce_scatter | solution.py:120
  520.7 60.9 %reduce-scatter.3.cloned.1.call-done = f32[144,1152]{1,0:T(8,128)} async-done(((f32[1152,1152]{1,0:T(8,128)}), f32[144,1152]{1,0:T(8,128)}) %reduce-scatter.3.cloned.1.call-update) | async-done | bytes 663568 | tf_op jit(solution)/shard_map/reduce_scatter | solution.py:120
  (131 shorter events, 22.4 us)
Async XLA Ops:
  7.2 14.0 %copy-start = (bf16[1000,1152]{1,0:T(8,128)(2,1)S(1)}, bf16[1000,1152]{1,0:T(8,128)(2,1)}, u32[]{:S(2)}) copy-start(bf16[1000,1152]{1,0:T(8,128)(2,1)} %param.19) | copy-start | bytes 6912004
  7.2 20.4 %copy-start.26 = (s32[3]{0:T(128)S(1)}, s32[3]{0:T(128)}, u32[]{:S(2)}) copy-start(s32[3]{0:T(128)} %param.17) | copy-start | bytes 40
  7.2 16.6 %copy-start.10 = (bf16[144,3,288]{2,0,1:T(8,128)(2,1)S(1)}, bf16[144,3,288]{2,0,1:T(8,128)(2,1)}, u32[]{:S(2)}) copy-start(bf16[144,3,288]{2,0,1:T(8,128)(2,1)} %param.26) | copy-start | bytes 746500
  7.2 21.0 %copy-start.27 = (s32[3]{0:T(128)S(1)}, s32[3]{0:T(128)}, u32[]{:S(2)}) copy-start(s32[3]{0:T(128)} %param.18) | copy-start | bytes 40
  7.2 21.0 %copy-start.19 = (f32[3,32,128]{2,1,0:T(8,128)S(1)}, f32[3,32,128]{2,1,0:T(8,128)}, u32[]{:S(2)}) copy-start(f32[3,32,128]{2,1,0:T(8,128)} %param.15) | copy-start | bytes 147460
  7.2 70.5 %all-reduce.13.cloned.1.call-start = ((), (), s32[]{:S(2)}) async-start(), calls=%async_computation.9 | async-start | bytes 663552
  24.8 158.6 %all-gather.10.cloned.1.call-start = ((), (), s32[]{:S(2)}) async-start(), calls=%async_computation.4 | async-start | bytes 2985984 | tf_op jit(solution)/shard_map/all_gather | solution.py:179
  25.6 157.8 %all-gather.12.cloned.1.call-start = ((), (), s32[]{:S(2)}) async-start(), calls=%async_computation.5 | async-start | bytes 2985984 | tf_op jit(solution)/shard_map/all_gather | solution.py:180
  26.3 170.5 %all-gather.6.cloned.1.call-start = ((), (), s32[]{:S(2)}) async-start(), calls=%async_computation.2 | async-start | bytes 2985984 | tf_op jit(solution)/shard_map/all_gather | solution.py:217
  26.9 179.4 %all-gather.8.cloned.1.call-start = ((), (), s32[]{:S(2)}) async-start(), calls=%async_computation.3 | async-start | bytes 2985984 | tf_op jit(solution)/shard_map/all_gather | solution.py:221
  27.5 256.5 %all-reduce.11.cloned.1.call-start = ((), (), s32[]{:S(2)}) async-start(), calls=%async_computation.6 | async-start | bytes 3538944 | tf_op jit(solution)/shard_map/psum | solution.py:109
  28.2 1.7 copy-start.23
  34.1 3.3 copy-start.4
  34.1 3.3 copy-start.7
  34.1 3.3 copy-start.20
  36.3 3.6 copy-start.21
  39.9 0.6 copy-start.22
  193.0 245.1 %all-reduce.15.cloned.1.call-start = ((), (), s32[]{:S(2)}) async-start(), calls=%async_computation.10 | async-start | bytes 7077888 | tf_op jit(solution)/shard_map/psum | solution.py:109
  284.0 2.2 copy-start.6
  284.0 2.2 copy-start.12
  287.0 0.8 copy-start.15
  288.5 0.9 copy-start.9
  290.3 2.6 copy-start.17
  290.3 2.6 copy-start.18
  305.1 215.6 %reduce-scatter.5.cloned.1.call-start = ((), (), s32[]{:S(2)}) async-start(), calls=%async_computation.8 | async-start | bytes 5971968 | tf_op jit(solution)/shard_map/reduce_scatter | solution.py:120
  441.2 1.9 copy-start.2
  441.7 1.8 copy-start.14
  446.6 2.2 copy-start.5
  446.6 2.2 copy-start.11
  449.6 0.8 copy-start.16
  449.6 1.5 copy-start.24
  449.6 1.5 copy-start.25
  452.3 4.7 copy-start.3
  452.3 4.7 copy-start.13
  457.0 2.6 copy-start.28
  458.3 1.2 copy-start.8
  464.7 116.9 %reduce-scatter.3.cloned.1.call-start = ((), (), s32[]{:S(2)}) async-start(), calls=%async_computation.7 | async-start | bytes 5971968 | tf_op jit(solution)/shard_map/reduce_scatter | solution.py:120
  465.0 116.6 %copy-start.1 = (bf16[1000,1152]{1,0:T(8,128)(2,1)S(1)}, bf16[1000,1152]{1,0:T(8,128)(2,1)}, u32[]{:S(2)}) copy-start(bf16[1000,1152]{1,0:T(8,128)(2,1)} %param.19) | copy-start | bytes 6912004
Sparse Core Ops, SparseCore 0:
  24.9 52.7 all-reduce.12
  79.6 30.7 all-gather.9
  112.3 30.1 all-gather.11
  144.2 30.1 all-gather.5
  176.1 30.1 all-gather.7
  208.5 75.4 all-reduce.10
  305.2 132.8 all-reduce.14
  464.8 55.8 reduce-scatter.4
  524.7 56.8 reduce-scatter.2
